TPU v7x, 512 devices: a whole 4x8x8 slice. The times are simulated.
512 devices in a mesh: row: 64 (over y, x, core), col: 8 (over z).
Axes of the slice: x: 4, y: 8, z: 8, core: 2. Of those that a mesh axis runs over, the one named last changes fastest.
Arguments:
- matrix: float32 [32768, 4096], P('row', 'col'), may hold values from -6 to 6
- first_leaves: float32 [32768, 256], P('row', 'col'), may hold values from -0.25 to 0.25
- first_factors: float32 [16384, 256], P('row', 'col'), may hold values from -0.1875 to 0.1875
- first_merges: float32 [16384, 256], P('row', 'col'), may hold values from -0.375 to 0.375
- first_mixers: float32 [16384, 256], P('row', 'col'), may hold values from -0.1875 to 0.1875
- second_leaves: float32 [32768, 256], P('row', 'col'), may hold values from -0.25 to 0.25
- second_factors: float32 [16384, 256], P('row', 'col'), may hold values from -0.1875 to 0.1875
- second_merges: float32 [16384, 256], P('row', 'col'), may hold values from -0.375 to 0.375
- second_mixers: float32 [16384, 256], P('row', 'col'), may hold values from -0.1875 to 0.1875
Outputs:
- updated: float32 [32768, 4096], P('row', 'col')
All inputs are finite; a program needn't handle non-finite values.
Results may differ from a plain program's by a relative error of at most 0.0001.
Values sent between devices are 32-bit elements; how exact they have to be, the bound alone decides.
A program may use at most 64 MiB of HBM per device.

v0:
```python
import jax
import jax.numpy as jnp
from jax import lax
from jax.sharding import PartitionSpec as P


def partner(value, axis, distance):
    mask = 2**distance
    pairs = [(source, source ^ mask) for source in range(lax.axis_size(axis))]
    return lax.ppermute(value, axis, pairs)


def turned_gather(arrays, axis, dims):
    turned = [jnp.moveaxis(a, dim, 0) for a, dim in zip(arrays, dims)]
    both = jnp.concatenate([t.reshape(len(t), -1) for t in turned], axis=1)
    filled, at, finished = (lax.all_gather(both, axis, axis=0, tiled=True), 0, [])
    for t, dim in zip(turned, dims):
        piece = filled[:, at : at + t[0].size].reshape(-1, *t.shape[1:])
        finished.append(jnp.moveaxis(piece, 0, dim))
        at += t[0].size
    return tuple(finished)


def product(left, right):
    return jnp.dot(left, right, precision=lax.Precision.HIGHEST)


def leaf_vectors(supplied, offset):
    shape = supplied.shape
    row_index = lax.broadcasted_iota(jnp.int32, shape, 0) - offset
    col_index = lax.broadcasted_iota(jnp.int32, shape, 1)
    unit = jnp.where(row_index == col_index, 1.0, 0.0).astype(supplied.dtype)
    return jnp.where(row_index > col_index, supplied, unit)


def tree_level(matrix, offset, merge, mixer, level_index, device):
    panel_width = merge.shape[0]
    stride = 1 << level_index
    is_low = device % (2 * stride) == 0
    is_partner = device % (2 * stride) == stride
    top_rows = lax.dynamic_slice_in_dim(matrix, offset, panel_width, 0)
    folded = product(merge.T, top_rows)
    outgoing = jnp.where(is_low, top_rows, folded)
    received, far_mixer = partner((outgoing, mixer), "row", level_index)
    use_mixer = jnp.where(is_low, far_mixer, mixer)
    combined = jnp.where(is_low, top_rows + received, received + folded)
    weight = product(use_mixer.T, combined)
    changed = jnp.where(is_low, top_rows - weight, top_rows - product(merge, weight))
    updated = jnp.where(is_low | is_partner, changed, top_rows)
    return lax.dynamic_update_slice_in_dim(matrix, updated, offset, 0)


def local(
    matrix,
    first_leaves,
    first_factors,
    first_merges,
    first_mixers,
    second_leaves,
    second_factors,
    second_merges,
    second_mixers,
):
    gathered = turned_gather(
        (
            first_leaves,
            first_factors,
            first_merges,
            first_mixers,
            second_leaves,
            second_factors,
            second_merges,
            second_mixers,
        ),
        "col",
        (1, 1, 1, 1, 1, 1, 1, 1),
    )
    device = lax.axis_index("row")
    levels = lax.axis_size("row").bit_length() - 1
    panel_width = first_factors.shape[0]
    for panel_index in range(2):
        leaves, factors, merges, mixers = gathered[4 * panel_index : 4 * panel_index + 4]
        if panel_index == 1:
            offset = jnp.where(device == 0, panel_width, 0).astype(jnp.int32)
        else:
            offset = jnp.zeros((), jnp.int32)
        vectors = leaf_vectors(leaves, offset)
        factor = jnp.triu(factors)
        matrix = matrix - product(vectors, product(factor.T, product(vectors.T, matrix)))
        merge = jnp.triu(merges)
        mixer = jnp.triu(mixers)
        for level_index in range(levels):
            matrix = tree_level(matrix, offset, merge, mixer, level_index, device)
    return matrix


def solution(mesh):
    placed = (
        P("row", "col"),
        P("row", "col"),
        P("row", "col"),
        P("row", "col"),
        P("row", "col"),
        P("row", "col"),
        P("row", "col"),
        P("row", "col"),
        P("row", "col"),
    )
    return jax.shard_map(
        local, mesh=mesh, in_specs=placed, out_specs=P("row", "col"), check_vma=False
    )
```

profile of v0, /device:TPU:1, one launch (start us, length us, event | category | flops | bytes accessed | tf_op | source)
XLA Modules:
  0.0 427.7 jit_solution(9656632236368342657)
XLA Ops:
  13.6 47.9 %all-gather.2.cloned.1.call-done = f32[256,2560]{1,0:T(8,128)} async-done(((f32[32,2560]{1,0:T(8,128)}), f32[256,2560]{1,0:T(8,128)}) %all-gather.2.cloned.1.call-update) | async-done | bytes 2621456 | tf_op jit(solution)/shard_map/all_gather | solution.py:16
  61.5 2.6 fusion.72
  65.7 3.2 convolution_subtract_fusion.1
  68.9 2.8 slice_select_fusion
  71.7 5.7 %collective-permute-start.1 = (f32[256,512]{1,0:T(8,128)}, f32[256,512]{1,0:T(8,128)}, u32[]{:S(2)}, u32[]{:S(2)}) collective-permute-start(f32[256,512]{1,0:T(8,128)} %get-tuple-element.17), channel_id=1, source_target_pairs={{0,8},{8,0},{16,24},{24,16},{32,40},{40,32},{48,56},{56,48},{64,72... | collective-permute-start | bytes 1572872 | tf_op jit(solution)/shard_map/ppermute | solution.py:10
  77.5 1.9 collective-permute-start
  80.9 2.0 fusion.46
  86.6 3.1 collective-permute-start.3
  89.7 2.2 collective-permute-start.2
  91.9 15.7 %collective-permute-done.2 = f32[256,256]{0,1:T(8,128)S(1)} collective-permute-done((f32[256,256]{0,1:T(8,128)S(1)}, f32[256,256]{0,1:T(8,128)S(1)}, u32[]{:S(2)}, u32[]{:S(2)}) %collective-permute-start.2) | collective-permute-done | bytes 262176 | tf_op jit(solution)/shard_map/ppermute | solution.py:10
  107.7 2.0 fusion.42
  112.3 4.6 %collective-permute-start.5 = (f32[256,512]{1,0:T(8,128)}, f32[256,512]{1,0:T(8,128)}, u32[]{:S(2)}, u32[]{:S(2)}) collective-permute-start(f32[256,512]{1,0:T(8,128)} %get-tuple-element.13), channel_id=1, source_target_pairs={{0,32},{8,40},{16,48},{24,56},{32,0},{40,8},{48,16},{56,24},{64,96... | collective-permute-start | bytes 1572872 | tf_op jit(solution)/shard_map/ppermute | solution.py:10
  116.9 2.2 collective-permute-start.4
  119.1 14.9 %collective-permute-done.4 = f32[256,256]{0,1:T(8,128)S(1)} collective-permute-done((f32[256,256]{0,1:T(8,128)S(1)}, f32[256,256]{0,1:T(8,128)S(1)}, u32[]{:S(2)}, u32[]{:S(2)}) %collective-permute-start.4) | collective-permute-done | bytes 262176 | tf_op jit(solution)/shard_map/ppermute | solution.py:10
  134.0 2.0 fusion.38
  136.8 1.8 broadcast_select_fusion.2
  138.7 3.1 collective-permute-start.7
  141.8 2.4 collective-permute-start.6
  144.2 13.8 %collective-permute-done.6 = f32[256,256]{0,1:T(8,128)S(1)} collective-permute-done((f32[256,256]{0,1:T(8,128)S(1)}, f32[256,256]{0,1:T(8,128)S(1)}, u32[]{:S(2)}, u32[]{:S(2)}) %collective-permute-start.6) | collective-permute-done | bytes 262176 | tf_op jit(solution)/shard_map/ppermute | solution.py:10
  158.0 2.0 fusion.34
  162.6 4.0 collective-permute-start.9
  166.7 2.1 collective-permute-start.8
  168.9 32.2 %collective-permute-done.8 = f32[256,256]{0,1:T(8,128)S(1)} collective-permute-done((f32[256,256]{0,1:T(8,128)S(1)}, f32[256,256]{0,1:T(8,128)S(1)}, u32[]{:S(2)}, u32[]{:S(2)}) %collective-permute-start.8) | collective-permute-done | bytes 262176 | tf_op jit(solution)/shard_map/ppermute | solution.py:10
  201.0 2.0 fusion.30
  205.7 8.0 %collective-permute-start.11 = (f32[256,512]{1,0:T(8,128)}, f32[256,512]{1,0:T(8,128)}, u32[]{:S(2)}, u32[]{:S(2)}) collective-permute-start(f32[256,512]{1,0:T(8,128)} %get-tuple-element.7), channel_id=1, source_target_pairs={{0,256},{8,264},{16,272},{24,280},{32,288},{40,296},{48,304},{56,3... | collective-permute-start | bytes 1572872 | tf_op jit(solution)/shard_map/ppermute | solution.py:10
  213.7 1.9 collective-permute-start.10
  215.6 32.3 %collective-permute-done.10 = f32[256,256]{0,1:T(8,128)S(1)} collective-permute-done((f32[256,256]{0,1:T(8,128)S(1)}, f32[256,256]{0,1:T(8,128)S(1)}, u32[]{:S(2)}, u32[]{:S(2)}) %collective-permute-start.10) | collective-permute-done | bytes 262176 | tf_op jit(solution)/shard_map/ppermute | solution.py:10
  247.9 2.0 fusion.26
  251.5 2.4 fusion.75
  254.5 2.3 convolution_subtract_fusion
  257.5 3.5 collective-permute-start.13
  261.1 1.9 collective-permute-start.12
  266.7 3.1 collective-permute-start.15
  269.8 2.4 collective-permute-start.14
  272.2 15.3 %collective-permute-done.14 = f32[256,256]{0,1:T(8,128)S(1)} collective-permute-done((f32[256,256]{0,1:T(8,128)S(1)}, f32[256,256]{0,1:T(8,128)S(1)}, u32[]{:S(2)}, u32[]{:S(2)}) %collective-permute-start.14) | collective-permute-done | bytes 262176 | tf_op jit(solution)/shard_map/ppermute | solution.py:10
  289.7 4.6 %collective-permute-start.17 = (f32[256,512]{1,0:T(8,128)S(1)}, f32[256,512]{1,0:T(8,128)S(1)}, u32[]{:S(2)}, u32[]{:S(2)}) collective-permute-start(f32[256,512]{1,0:T(8,128)S(1)} %get-tuple-element.28), channel_id=1, source_target_pairs={{0,32},{8,40},{16,48},{24,56},{32,0},{40,8},{48,16},{56,24},{64,96... | collective-permute-start | bytes 1572872 | tf_op jit(solution)/shard_map/ppermute | solution.py:10
  294.3 2.2 collective-permute-start.16
  296.5 14.7 %collective-permute-done.16 = f32[256,256]{0,1:T(8,128)S(1)} collective-permute-done((f32[256,256]{0,1:T(8,128)S(1)}, f32[256,256]{0,1:T(8,128)S(1)}, u32[]{:S(2)}, u32[]{:S(2)}) %collective-permute-start.16) | collective-permute-done | bytes 262176 | tf_op jit(solution)/shard_map/ppermute | solution.py:10
  313.4 1.9 collective-permute-start.19
  315.3 3.4 collective-permute-start.18
  318.7 13.8 %collective-permute-done.18 = f32[256,256]{0,1:T(8,128)S(1)} collective-permute-done((f32[256,256]{0,1:T(8,128)S(1)}, f32[256,256]{0,1:T(8,128)S(1)}, u32[]{:S(2)}, u32[]{:S(2)}) %collective-permute-start.18) | collective-permute-done | bytes 262176 | tf_op jit(solution)/shard_map/ppermute | solution.py:10
  334.7 2.4 collective-permute-start.21
  337.2 3.7 collective-permute-start.20
  340.9 32.9 %collective-permute-done.20 = f32[256,256]{0,1:T(8,128)S(1)} collective-permute-done((f32[256,256]{0,1:T(8,128)S(1)}, f32[256,256]{0,1:T(8,128)S(1)}, u32[]{:S(2)}, u32[]{:S(2)}) %collective-permute-start.20) | collective-permute-done | bytes 262176 | tf_op jit(solution)/shard_map/ppermute | solution.py:10
  376.0 4.4 %collective-permute-start.23 = (f32[256,512]{1,0:T(8,128)S(1)}, f32[256,512]{1,0:T(8,128)S(1)}, u32[]{:S(2)}, u32[]{:S(2)}) collective-permute-start(f32[256,512]{1,0:T(8,128)S(1)} %get-tuple-element.34), channel_id=1, source_target_pairs={{0,256},{8,264},{16,272},{24,280},{32,288},{40,296},{48,304},{56,3... | collective-permute-start | bytes 1572872 | tf_op jit(solution)/shard_map/ppermute | solution.py:10
  380.4 4.8 %collective-permute-start.22 = (f32[256,256]{0,1:T(8,128)S(1)}, f32[256,256]{0,1:T(8,128)S(1)}, u32[]{:S(2)}, u32[]{:S(2)}) collective-permute-start(f32[256,256]{0,1:T(8,128)S(1)} %get-tuple-element.5), channel_id=1, source_target_pairs={{0,256},{8,264},{16,272},{24,280},{32,288},{40,296},{48,304},{56,3... | collective-permute-start | bytes 786440 | tf_op jit(solution)/shard_map/ppermute | solution.py:10
  385.3 32.3 %collective-permute-done.22 = f32[256,256]{0,1:T(8,128)S(1)} collective-permute-done((f32[256,256]{0,1:T(8,128)S(1)}, f32[256,256]{0,1:T(8,128)S(1)}, u32[]{:S(2)}, u32[]{:S(2)}) %collective-permute-start.22) | collective-permute-done | bytes 262176 | tf_op jit(solution)/shard_map/ppermute | solution.py:10
  418.9 2.0 select_dynamic-update-slice_fusion
  (88 shorter events, 38.6 us)
Async XLA Ops:
  6.5 54.9 %all-gather.2.cloned.1.call-start = ((), (), s32[]{:S(2)}) async-start(), calls=%async_computation | async-start | bytes 2949120 | tf_op jit(solution)/shard_map/all_gather | solution.py:16
  12.8 0.7 copy-start.12
  61.5 4.2 copy-start.1
  71.7 9.2 %collective-permute-start.1 = (f32[256,512]{1,0:T(8,128)}, f32[256,512]{1,0:T(8,128)}, u32[]{:S(2)}, u32[]{:S(2)}) collective-permute-start(f32[256,512]{1,0:T(8,128)} %get-tuple-element.17), channel_id=1, source_target_pairs={{0,8},{8,0},{16,24},{24,16},{32,40},{40,32},{48,56},{56,48},{64,72... | collective-permute-start | bytes 1572872 | tf_op jit(solution)/shard_map/ppermute | solution.py:10
  77.5 3.4 collective-permute-start
  84.8 1.8 copy-start.8
  86.6 21.1 %collective-permute-start.3 = (f32[256,512]{1,0:T(8,128)}, f32[256,512]{1,0:T(8,128)}, u32[]{:S(2)}, u32[]{:S(2)}) collective-permute-start(f32[256,512]{1,0:T(8,128)} %get-tuple-element.15), channel_id=1, source_target_pairs={{0,16},{8,24},{16,0},{24,8},{32,48},{40,56},{48,32},{56,40},{64,80... | collective-permute-start | bytes 1572872 | tf_op jit(solution)/shard_map/ppermute | solution.py:10
  89.7 18.0 %collective-permute-start.2 = (f32[256,256]{0,1:T(8,128)S(1)}, f32[256,256]{0,1:T(8,128)S(1)}, u32[]{:S(2)}, u32[]{:S(2)}) collective-permute-start(f32[256,256]{0,1:T(8,128)S(1)} %get-tuple-element.6), channel_id=1, source_target_pairs={{0,16},{8,24},{16,0},{24,8},{32,48},{40,56},{48,32},{56,40},{64,80... | collective-permute-start | bytes 786440 | tf_op jit(solution)/shard_map/ppermute | solution.py:10
  91.9 17.8 %copy-start.9 = (f32[256,512]{1,0:T(8,128)S(1)}, f32[256,512]{1,0:T(8,128)}, u32[]{:S(2)}) copy-start(f32[256,512]{1,0:T(8,128)} %copy-done.8) | copy-start | bytes 1572868
  110.5 1.8 copy-start.4
  112.3 21.7 %collective-permute-start.5 = (f32[256,512]{1,0:T(8,128)}, f32[256,512]{1,0:T(8,128)}, u32[]{:S(2)}, u32[]{:S(2)}) collective-permute-start(f32[256,512]{1,0:T(8,128)} %get-tuple-element.13), channel_id=1, source_target_pairs={{0,32},{8,40},{16,48},{24,56},{32,0},{40,8},{48,16},{56,24},{64,96... | collective-permute-start | bytes 1572872 | tf_op jit(solution)/shard_map/ppermute | solution.py:10
  116.9 17.1 %collective-permute-start.4 = (f32[256,256]{0,1:T(8,128)S(1)}, f32[256,256]{0,1:T(8,128)S(1)}, u32[]{:S(2)}, u32[]{:S(2)}) collective-permute-start(f32[256,256]{0,1:T(8,128)S(1)} %get-tuple-element.6), channel_id=1, source_target_pairs={{0,32},{8,40},{16,48},{24,56},{32,0},{40,8},{48,16},{56,24},{64,96... | collective-permute-start | bytes 786440 | tf_op jit(solution)/shard_map/ppermute | solution.py:10
  119.1 16.9 %copy-start.5 = (f32[256,512]{1,0:T(8,128)S(1)}, f32[256,512]{1,0:T(8,128)}, u32[]{:S(2)}) copy-start(f32[256,512]{1,0:T(8,128)} %copy-done.4) | copy-start | bytes 1572868
  136.8 1.8 copy-start.6
  138.7 19.3 %collective-permute-start.7 = (f32[256,512]{1,0:T(8,128)}, f32[256,512]{1,0:T(8,128)}, u32[]{:S(2)}, u32[]{:S(2)}) collective-permute-start(f32[256,512]{1,0:T(8,128)} %get-tuple-element.11), channel_id=1, source_target_pairs={{0,64},{8,72},{16,80},{24,88},{32,96},{40,104},{48,112},{56,120},{... | collective-permute-start | bytes 1572872 | tf_op jit(solution)/shard_map/ppermute | solution.py:10
  141.8 16.2 %collective-permute-start.6 = (f32[256,256]{0,1:T(8,128)S(1)}, f32[256,256]{0,1:T(8,128)S(1)}, u32[]{:S(2)}, u32[]{:S(2)}) collective-permute-start(f32[256,256]{0,1:T(8,128)S(1)} %get-tuple-element.6), channel_id=1, source_target_pairs={{0,64},{8,72},{16,80},{24,88},{32,96},{40,104},{48,112},{56,120},{... | collective-permute-start | bytes 786440 | tf_op jit(solution)/shard_map/ppermute | solution.py:10
  144.1 15.9 %copy-start.7 = (f32[256,512]{1,0:T(8,128)S(1)}, f32[256,512]{1,0:T(8,128)}, u32[]{:S(2)}) copy-start(f32[256,512]{1,0:T(8,128)} %copy-done.6) | copy-start | bytes 1572868
  160.8 1.8 copy-start.2
  162.6 38.4 %collective-permute-start.9 = (f32[256,512]{1,0:T(8,128)}, f32[256,512]{1,0:T(8,128)}, u32[]{:S(2)}, u32[]{:S(2)}) collective-permute-start(f32[256,512]{1,0:T(8,128)} %get-tuple-element.9), channel_id=1, source_target_pairs={{0,128},{8,136},{16,144},{24,152},{32,160},{40,168},{48,176},{56,1... | collective-permute-start | bytes 1572872 | tf_op jit(solution)/shard_map/ppermute | solution.py:10
  166.7 34.4 %collective-permute-start.8 = (f32[256,256]{0,1:T(8,128)S(1)}, f32[256,256]{0,1:T(8,128)S(1)}, u32[]{:S(2)}, u32[]{:S(2)}) collective-permute-start(f32[256,256]{0,1:T(8,128)S(1)} %get-tuple-element.6), channel_id=1, source_target_pairs={{0,128},{8,136},{16,144},{24,152},{32,160},{40,168},{48,176},{56,1... | collective-permute-start | bytes 786440 | tf_op jit(solution)/shard_map/ppermute | solution.py:10
  168.9 34.2 %copy-start.3 = (f32[256,512]{1,0:T(8,128)S(1)}, f32[256,512]{1,0:T(8,128)}, u32[]{:S(2)}) copy-start(f32[256,512]{1,0:T(8,128)} %copy-done.2) | copy-start | bytes 1572868
  203.8 1.8 copy-start.10
  205.7 42.3 %collective-permute-start.11 = (f32[256,512]{1,0:T(8,128)}, f32[256,512]{1,0:T(8,128)}, u32[]{:S(2)}, u32[]{:S(2)}) collective-permute-start(f32[256,512]{1,0:T(8,128)} %get-tuple-element.7), channel_id=1, source_target_pairs={{0,256},{8,264},{16,272},{24,280},{32,288},{40,296},{48,304},{56,3... | collective-permute-start | bytes 1572872 | tf_op jit(solution)/shard_map/ppermute | solution.py:10
  213.7 34.3 %collective-permute-start.10 = (f32[256,256]{0,1:T(8,128)S(1)}, f32[256,256]{0,1:T(8,128)S(1)}, u32[]{:S(2)}, u32[]{:S(2)}) collective-permute-start(f32[256,256]{0,1:T(8,128)S(1)} %get-tuple-element.6), channel_id=1, source_target_pairs={{0,256},{8,264},{16,272},{24,280},{32,288},{40,296},{48,304},{56,3... | collective-permute-start | bytes 786440 | tf_op jit(solution)/shard_map/ppermute | solution.py:10
  215.6 34.4 %copy-start.11 = (f32[256,512]{1,0:T(8,128)S(1)}, f32[256,512]{1,0:T(8,128)}, u32[]{:S(2)}) copy-start(f32[256,512]{1,0:T(8,128)} %copy-done.10) | copy-start | bytes 1572868
  257.5 7.0 %collective-permute-start.13 = (f32[256,512]{1,0:T(8,128)S(1)}, f32[256,512]{1,0:T(8,128)S(1)}, u32[]{:S(2)}, u32[]{:S(2)}) collective-permute-start(f32[256,512]{1,0:T(8,128)S(1)} %get-tuple-element.24), channel_id=1, source_target_pairs={{0,8},{8,0},{16,24},{24,16},{32,40},{40,32},{48,56},{56,48},{64,72... | collective-permute-start | bytes 1572872 | tf_op jit(solution)/shard_map/ppermute | solution.py:10
  261.1 3.4 collective-permute-start.12
  266.7 20.9 %collective-permute-start.15 = (f32[256,512]{1,0:T(8,128)S(1)}, f32[256,512]{1,0:T(8,128)S(1)}, u32[]{:S(2)}, u32[]{:S(2)}) collective-permute-start(f32[256,512]{1,0:T(8,128)S(1)} %get-tuple-element.26), channel_id=1, source_target_pairs={{0,16},{8,24},{16,0},{24,8},{32,48},{40,56},{48,32},{56,40},{64,80... | collective-permute-start | bytes 1572872 | tf_op jit(solution)/shard_map/ppermute | solution.py:10
  269.8 17.7 %collective-permute-start.14 = (f32[256,256]{0,1:T(8,128)S(1)}, f32[256,256]{0,1:T(8,128)S(1)}, u32[]{:S(2)}, u32[]{:S(2)}) collective-permute-start(f32[256,256]{0,1:T(8,128)S(1)} %get-tuple-element.5), channel_id=1, source_target_pairs={{0,16},{8,24},{16,0},{24,8},{32,48},{40,56},{48,32},{56,40},{64,80... | collective-permute-start | bytes 786440 | tf_op jit(solution)/shard_map/ppermute | solution.py:10
  289.7 21.5 %collective-permute-start.17 = (f32[256,512]{1,0:T(8,128)S(1)}, f32[256,512]{1,0:T(8,128)S(1)}, u32[]{:S(2)}, u32[]{:S(2)}) collective-permute-start(f32[256,512]{1,0:T(8,128)S(1)} %get-tuple-element.28), channel_id=1, source_target_pairs={{0,32},{8,40},{16,48},{24,56},{32,0},{40,8},{48,16},{56,24},{64,96... | collective-permute-start | bytes 1572872 | tf_op jit(solution)/shard_map/ppermute | solution.py:10
  294.3 16.9 %collective-permute-start.16 = (f32[256,256]{0,1:T(8,128)S(1)}, f32[256,256]{0,1:T(8,128)S(1)}, u32[]{:S(2)}, u32[]{:S(2)}) collective-permute-start(f32[256,256]{0,1:T(8,128)S(1)} %get-tuple-element.5), channel_id=1, source_target_pairs={{0,32},{8,40},{16,48},{24,56},{32,0},{40,8},{48,16},{56,24},{64,96... | collective-permute-start | bytes 786440 | tf_op jit(solution)/shard_map/ppermute | solution.py:10
  313.4 19.1 %collective-permute-start.19 = (f32[256,512]{1,0:T(8,128)S(1)}, f32[256,512]{1,0:T(8,128)S(1)}, u32[]{:S(2)}, u32[]{:S(2)}) collective-permute-start(f32[256,512]{1,0:T(8,128)S(1)} %get-tuple-element.30), channel_id=1, source_target_pairs={{0,64},{8,72},{16,80},{24,88},{32,96},{40,104},{48,112},{56,120},{... | collective-permute-start | bytes 1572872 | tf_op jit(solution)/shard_map/ppermute | solution.py:10
  315.3 17.2 %collective-permute-start.18 = (f32[256,256]{0,1:T(8,128)S(1)}, f32[256,256]{0,1:T(8,128)S(1)}, u32[]{:S(2)}, u32[]{:S(2)}) collective-permute-start(f32[256,256]{0,1:T(8,128)S(1)} %get-tuple-element.5), channel_id=1, source_target_pairs={{0,64},{8,72},{16,80},{24,88},{32,96},{40,104},{48,112},{56,120},{... | collective-permute-start | bytes 786440 | tf_op jit(solution)/shard_map/ppermute | solution.py:10
  334.7 39.1 %collective-permute-start.21 = (f32[256,512]{1,0:T(8,128)S(1)}, f32[256,512]{1,0:T(8,128)S(1)}, u32[]{:S(2)}, u32[]{:S(2)}) collective-permute-start(f32[256,512]{1,0:T(8,128)S(1)} %get-tuple-element.32), channel_id=1, source_target_pairs={{0,128},{8,136},{16,144},{24,152},{32,160},{40,168},{48,176},{56,1... | collective-permute-start | bytes 1572872 | tf_op jit(solution)/shard_map/ppermute | solution.py:10
  337.2 36.6 %collective-permute-start.20 = (f32[256,256]{0,1:T(8,128)S(1)}, f32[256,256]{0,1:T(8,128)S(1)}, u32[]{:S(2)}, u32[]{:S(2)}) collective-permute-start(f32[256,256]{0,1:T(8,128)S(1)} %get-tuple-element.5), channel_id=1, source_target_pairs={{0,128},{8,136},{16,144},{24,152},{32,160},{40,168},{48,176},{56,1... | collective-permute-start | bytes 786440 | tf_op jit(solution)/shard_map/ppermute | solution.py:10
  375.4 43.5 %copy-start = (f32[512,512]{1,0:T(8,128)}, f32[512,512]{1,0:T(8,128)S(1)}, u32[]{:S(2)}) copy-start(f32[512,512]{1,0:T(8,128)S(1)} %select_dynamic-update-slice_fusion.1) | copy-start | bytes 3145732
  376.0 41.5 %collective-permute-start.23 = (f32[256,512]{1,0:T(8,128)S(1)}, f32[256,512]{1,0:T(8,128)S(1)}, u32[]{:S(2)}, u32[]{:S(2)}) collective-permute-start(f32[256,512]{1,0:T(8,128)S(1)} %get-tuple-element.34), channel_id=1, source_target_pairs={{0,256},{8,264},{16,272},{24,280},{32,288},{40,296},{48,304},{56,3... | collective-permute-start | bytes 1572872 | tf_op jit(solution)/shard_map/ppermute | solution.py:10
  380.4 37.1 %collective-permute-start.22 = (f32[256,256]{0,1:T(8,128)S(1)}, f32[256,256]{0,1:T(8,128)S(1)}, u32[]{:S(2)}, u32[]{:S(2)}) collective-permute-start(f32[256,256]{0,1:T(8,128)S(1)} %get-tuple-element.5), channel_id=1, source_target_pairs={{0,256},{8,264},{16,272},{24,280},{32,288},{40,296},{48,304},{56,3... | collective-permute-start | bytes 786440 | tf_op jit(solution)/shard_map/ppermute | solution.py:10
Sparse Core Ops, SparseCore 0:
  13.7 47.7 all-gather.1
where the time goes:
time: 429 us; the launch traced here: 428 us
  waiting for transfers between devices  269 us (63%)
  starting transfers between devices  79.6 us (19%)
  matrix products  54.9 us (13%)
  between operations  14.2 us (3%)
  local copies, waits for them, and re-layouts  7.03 us (2%)
    ppermute x24, waiting for transfers between devices, partner(): return lax.ppermute(value, axis, pairs)  221 us
    ppermute x24, starting transfers between devices, partner(): return lax.ppermute(value, axis, pairs)  79.6 us
    dot_general x42, matrix products, product(): return jnp.dot(left, right, precision=lax.Precision.HIGHEST)  54.9 us
    all_gather x1, waiting for transfers between devices, turned_gather(): lax.all_gather(both, axis, axis=0, tiled=True)  47.9 us
  transfers between devices with their start and end apart: 25, of which 13 were waited for; matrix products, arithmetic and copies ran while one was open for 0% of the time, Pallas kernels for 0%

commit v1 on v0

v1 whole, which is shorter than its diff:
```python
import functools

import jax
import jax.numpy as jnp
from jax import lax
from jax.experimental import pallas as pl
from jax.experimental.pallas import tpu as pltpu
from jax.sharding import PartitionSpec as P

LANES = 128
MESH = pl.DeviceIdType.MESH
F32 = jnp.float32
BF16 = jnp.bfloat16


def halves(value):
    high = value.astype(BF16)
    return high, (value - high.astype(F32)).astype(BF16)


def left_operand(value):
    high, low = halves(value)
    return jnp.concatenate([high, high, low], axis=1)


def times(operator, value):
    high, low = halves(value)
    right = jnp.concatenate([high, low, high], axis=0)
    return jnp.dot(operator[...], right, preferred_element_type=F32)


def lower_triangle(value):
    row = lax.broadcasted_iota(jnp.int32, value.shape, 0)
    col = lax.broadcasted_iota(jnp.int32, value.shape, 1)
    return jnp.where(col <= row, value, 0.0)


def kernel(
    levels,
    ring_size,
    matrix,
    v1,
    f1,
    u1,
    g1,
    v2,
    f2,
    u2,
    g2,
    out,
    x,
    leafs,
    trees,
    far_mixers,
    tops,
    far_folds,
    folds,
    far_tops,
    op_v,
    op_vt,
    op_f,
    op_u,
    op_ut,
    op_g,
    op_far,
    load_sem,
    x_sem,
    out_sem,
    ring_send,
    ring_recv,
    fold_send,
    fold_recv,
    top_send,
    top_recv,
    mixer_send,
    mixer_recv,
):
    chunks, rows, _ = x.shape
    width = trees.shape[1]
    share = width // ring_size
    half = ring_size // 2

    d = lax.axis_index("row")
    k = lax.axis_index("col")
    right = lax.rem(k + 1, ring_size)
    left = lax.rem(k + ring_size - 1, ring_size)
    steps = jnp.int32(0)
    reach = jnp.int32(1)
    for i in range(levels):
        one = jnp.where(lax.rem(d, 2 ** (i + 1)) == 0, 1, 0)
        steps = steps + one
        reach = reach + one * 2**i
    not_root = d != 0
    parent = d - reach

    own = pl.ds(pl.multiple_of(k * share, share), share)
    loads = []
    for p, (v, f, u, g) in enumerate(((v1, f1, u1, g1), (v2, f2, u2, g2))):
        places = (
            (v, leafs.at[p, own, pl.ds(0, rows)]),
            (f, leafs.at[p, own, pl.ds(rows, width)]),
            (u, trees.at[p, own, pl.ds(0, width)]),
            (g, trees.at[p, own, pl.ds(width, width)]),
        )
        for i, (source, place) in enumerate(places):
            loads.append(pltpu.make_async_copy(source, place, load_sem.at[p, i]))
    x_loads = [
        pltpu.make_async_copy(
            matrix.at[:, pl.ds(c * LANES, LANES)], x.at[c], x_sem.at[c]
        )
        for c in range(chunks)
    ]
    for copy in loads[:4] + x_loads + loads[4:]:
        copy.start()

    barrier = pltpu.get_barrier_semaphore()

    def greet(row, col):
        pl.semaphore_signal(barrier, inc=1, device_id=(row, col), device_id_type=MESH)

    greet(d, left)
    greet(d, right)

    def greet_lower(i, stride):
        greet(d + stride, k)
        return stride * 2

    lax.fori_loop(0, steps, greet_lower, jnp.int32(1))

    @pl.when(not_root)
    def _():
        greet(parent, k)

    pl.semaphore_wait(barrier, 2 + steps + jnp.where(not_root, 1, 0))

    def hops(piece, way):
        return half if piece == way else half - 1

    def ring_copy(p, piece, way, hop, sent):
        back = hop - 1 if sent else hop
        shard = lax.rem(k + (ring_size - back if way == 0 else back), ring_size)
        row = pl.ds(pl.multiple_of(shard * share, share), share)
        if piece == 0:
            first = pl.multiple_of(((shard * share) // LANES) * LANES, LANES)
            ref = leafs.at[p, row, pl.ds(first, rows + LANES)]
        else:
            ref = trees.at[p, row, :]
        return pltpu.make_async_remote_copy(
            src_ref=ref,
            dst_ref=ref,
            send_sem=ring_send.at[p, piece, way, hop - 1],
            recv_sem=ring_recv.at[p, piece, way, hop - 1],
            device_id=(d, right if way == 0 else left),
            device_id_type=MESH,
        )

    def relay(p, hop):
        for piece in range(2):
            for way in range(2):
                if hop <= hops(piece, way):
                    if hop > 1:
                        ring_copy(p, piece, way, hop - 1, False).wait_recv()
                    ring_copy(p, piece, way, hop, True).start()

    def gathered(p, piece):
        for way in range(2):
            if hops(piece, way) > 0:
                ring_copy(p, piece, way, hops(piece, way), False).wait_recv()

    def top_copy(p, level, c, stride):
        return pltpu.make_async_remote_copy(
            src_ref=tops.at[p, level, c],
            dst_ref=far_tops.at[p, c],
            send_sem=top_send.at[p, level, c],
            recv_sem=top_recv.at[p, c],
            device_id=(d + stride, k),
            device_id_type=MESH,
        )

    def fold_copy(p, c, level):
        return pltpu.make_async_remote_copy(
            src_ref=folds.at[p, c],
            dst_ref=far_folds.at[p, level, c],
            send_sem=fold_send.at[p, c],
            recv_sem=fold_recv.at[p, level, c],
            device_id=(parent, k),
            device_id_type=MESH,
        )

    def mixer_copy(p, level):
        return pltpu.make_async_remote_copy(
            src_ref=trees.at[p, :, pl.ds(width, width)],
            dst_ref=far_mixers.at[p, level],
            send_sem=mixer_send.at[p],
            recv_sem=mixer_recv.at[p, level],
            device_id=(parent, k),
            device_id_type=MESH,
        )

    def fold(p, c):
        folds[p, c] = times(op_ut, tops[p, steps, c])
        fold_copy(p, c, steps).start()

    def each_chunk(body):
        def step(c, carry):
            body(c)
            return carry

        lax.fori_loop(0, chunks, step, 0)

    def prepare_leaf(p, offset):
        raw = leafs[p, :, pl.ds(0, rows)]
        row = lax.broadcasted_iota(jnp.int32, raw.shape, 1) - offset
        col = lax.broadcasted_iota(jnp.int32, raw.shape, 0)
        vectors = jnp.where(row > col, raw, jnp.where(row == col, 1.0, 0.0))
        op_vt[...] = left_operand(vectors)
        op_v[...] = left_operand(vectors.T)
        op_f[...] = left_operand(lower_triangle(leafs[p, :, pl.ds(rows, width)]))

    def prepare_tree(p):
        merge = lower_triangle(trees[p, :, pl.ds(0, width)])
        op_ut[...] = left_operand(merge)
        op_u[...] = left_operand(merge.T)
        op_g[...] = left_operand(lower_triangle(trees[p, :, pl.ds(width, width)]))

    def panel(p, offset):
        block = pl.ds(pl.multiple_of(offset, width), width)
        gathered(p, 0)
        prepare_leaf(p, offset)
        if p == 0:
            for copy in x_loads:
                copy.wait()

        def leaf(c):
            before = x[c]
            mixed = times(op_f, times(op_vt, before))
            x[c] = before - times(op_v, mixed)
            tops[p, 0, c] = x[c, block, :]

            @pl.when(steps > 0)
            def _():
                top_copy(p, 0, c, 1).start()

        each_chunk(leaf)
        gathered(p, 1)

        @pl.when(not_root)
        def _():
            mixer_copy(p, steps).start()

        prepare_tree(p)

        @pl.when(steps == 0)
        def _():
            each_chunk(functools.partial(fold, p))

        def level_step(level, stride):
            mixer_copy(p, level).wait_recv()
            op_far[...] = left_operand(lower_triangle(far_mixers[p, level]))

            def upper(c):
                fold_copy(p, c, level).wait_recv()
                before = tops[p, level, c]
                weight = times(op_far, before + far_folds[p, level, c])
                tops[p, level + 1, c] = before - weight

                @pl.when(level + 1 < steps)
                def _():
                    top_copy(p, level + 1, c, stride * 2).start()

                @pl.when((level + 1 == steps) & not_root)
                def _():
                    fold(p, c)

            each_chunk(upper)
            if p == 0:
                for hop in range(2, half + 1):

                    @pl.when(level == hop - 2)
                    def _():
                        relay(1, hop)

            return stride * 2

        lax.fori_loop(0, steps, level_step, jnp.int32(1))

        def lower(c):
            top_copy(p, 0, c, 0).wait_recv()
            weight = times(op_g, far_tops[p, c] + folds[p, c])
            x[c, pl.ds(0, width), :] = tops[p, steps, c] - times(op_u, weight)

        def root(c):
            x[c, block, :] = tops[p, levels, c]

        @pl.when(not_root)
        def _():
            each_chunk(lower)

        @pl.when(d == 0)
        def _():
            each_chunk(root)

        if p == 0:
            for hop in range(2, half + 1):

                @pl.when(steps <= hop - 2)
                def _():
                    relay(1, hop)

    for copy in loads[:4]:
        copy.wait()
    for hop in range(1, half + 1):
        relay(0, hop)
    for copy in loads[4:]:
        copy.wait()
    relay(1, 1)
    panel(0, jnp.int32(0))
    panel(1, jnp.where(d == 0, width, 0))

    stores = [
        pltpu.make_async_copy(
            x.at[c], out.at[:, pl.ds(c * LANES, LANES)], out_sem.at[c]
        )
        for c in range(chunks)
    ]
    for copy in stores:
        copy.start()

    for p in range(2):
        for piece in range(2):
            for way in range(2):
                for hop in range(1, hops(piece, way) + 1):
                    ring_copy(p, piece, way, hop, True).wait_send()

        def sent_tops(level, carry):
            each_chunk(lambda c: top_copy(p, level, c, 0).wait_send())
            return carry

        lax.fori_loop(0, steps, sent_tops, 0)

        @pl.when(not_root)
        def _():
            mixer_copy(p, steps).wait_send()
            each_chunk(lambda c: fold_copy(p, c, steps).wait_send())

    for copy in stores:
        copy.wait()


def local(levels, ring_size, matrix, *reflectors):
    rows, cols = matrix.shape
    turned = [r.T for r in reflectors]
    width = turned[1].shape[1]
    chunks = cols // LANES
    half = ring_size // 2
    vmem, dma = pltpu.VMEM, pltpu.SemaphoreType.DMA
    anywhere = pl.BlockSpec(memory_space=pl.ANY)
    tile = (chunks, width, LANES)
    flops = 2 * 3 * 2 * cols * width * (3 * rows + 9 * width)
    return pl.pallas_call(
        functools.partial(kernel, levels, ring_size),
        out_shape=jax.ShapeDtypeStruct(matrix.shape, matrix.dtype),
        in_specs=[anywhere] * 9,
        out_specs=anywhere,
        scratch_shapes=[
            vmem((chunks, rows, LANES), F32),
            vmem((2, width, rows + width), F32),
            vmem((2, width, 2 * width), F32),
            vmem((2, levels, width, width), F32),
            vmem((2, levels + 1, *tile), F32),
            vmem((2, levels, *tile), F32),
            vmem((2, *tile), F32),
            vmem((2, *tile), F32),
            vmem((rows, 3 * width), BF16),
            vmem((width, 3 * rows), BF16),
            vmem((width, 3 * width), BF16),
            vmem((width, 3 * width), BF16),
            vmem((width, 3 * width), BF16),
            vmem((width, 3 * width), BF16),
            vmem((width, 3 * width), BF16),
            dma((2, 4)),
            dma((chunks,)),
            dma((chunks,)),
            dma((2, 2, 2, half)),
            dma((2, 2, 2, half)),
            dma((2, chunks)),
            dma((2, levels, chunks)),
            dma((2, levels, chunks)),
            dma((2, chunks)),
            dma((2,)),
            dma((2, levels)),
        ],
        compiler_params=pltpu.CompilerParams(
            collective_id=0, has_side_effects=True, vmem_limit_bytes=48 * 2**20
        ),
        cost_estimate=pl.CostEstimate(
            flops=flops, bytes_accessed=8 * rows * cols, transcendentals=0
        ),
        name="tree_update",
    )(matrix, *turned)


def solution(mesh):
    levels = mesh.shape["row"].bit_length() - 1
    placed = P("row", "col")
    return jax.shard_map(
        functools.partial(local, levels, mesh.shape["col"]),
        mesh=mesh,
        in_specs=(placed,) * 9,
        out_specs=placed,
        check_vma=False,
    )
```

time: 429 us -> 111 us (0.26)
  the two profiles are of different devices: /device:TPU:1 before, /device:TPU:32 now
where the time goes in v1:
time: 111 us; the launch traced here: 110 us
  Pallas kernels  102 us (92%)
  local copies, waits for them, and re-layouts  8.42 us (8%)
    pallas_call x1, Pallas kernels, local(): pl.pallas_call(functools.partial(kernel, levels, ring_size), out_shape=ja...  102 us
    unnamed x19, local copies, waits for them, and re-layouts  8.42 us

profile of v1, /device:TPU:32, one launch (start us, length us, event | category | flops | bytes accessed | tf_op | source)
XLA Modules:
  0.0 110.0 jit_solution(14409652602126459945)
XLA Ops:
  0.0 0.0 copy-start
  0.0 1.2 %copy-done = f32[512,512]{1,0:T(8,128)S(1)} copy-done((f32[512,512]{1,0:T(8,128)S(1)}, f32[512,512]{1,0:T(8,128)}, u32[]{:S(2)}) %copy-start) | copy-done | bytes 1048600
  1.2 0.0 copy-start.1
  1.2 0.8 copy-done.1
  2.1 0.0 copy-start.2
  2.1 0.8 copy-done.2
  2.9 0.0 copy-start.3
  2.9 0.8 copy-done.3
  3.7 0.0 copy-start.4
  3.7 0.8 copy-done.4
  4.4 0.0 copy-start.5
  4.4 0.8 copy-done.5
  5.2 0.0 copy-start.6
  5.2 0.8 copy-done.6
  5.9 0.0 copy-start.7
  5.9 0.8 copy-done.7
  6.7 0.0 copy-start.8
  6.7 0.8 copy-done.8
  7.5 101.6 %tree_update.1 = f32[512,512]{1,0:T(8,128)S(1)} custom-call(f32[512,512]{1,0:T(8,128)S(1)} %copy-done, f32[32,512]{1,0:T(8,128)S(1)} %bitcast.8, f32[32,256]{1,0:T(8,128)S(1)} %bitcast.10, f32[32,256]{1,0:T(8,128)S(1)} %bitcast.11, f32[32,256]{1,0:T(8,128)S(1)} %bitcast.12, f32[32,512]{1,0:T(8,128)S(1)} %bitcast.9, f32[32,256]{1,0:T(8,128)S(1)} %bitcast.13, ...), custom_call_target="tpu_custom_call" | custom-call | flops 6039797760 | bytes 2097152 | tf_op jit(solution)/shard_map/tree_update/pallas_call | solution.py:360
  109.0 1.0 copy.11
Async XLA Ops:
  0.0 1.2 %copy-start = (f32[512,512]{1,0:T(8,128)S(1)}, f32[512,512]{1,0:T(8,128)}, u32[]{:S(2)}) copy-start(f32[512,512]{1,0:T(8,128)} %matrix.1) | copy-start | bytes 3145732
  1.2 0.8 copy-start.1
  2.1 0.8 copy-start.2
  2.9 0.8 copy-start.3
  3.7 0.8 copy-start.4
  4.4 0.8 copy-start.5
  5.2 0.8 copy-start.6
  5.9 0.8 copy-start.7
  6.7 0.8 copy-start.8

commit v2 on v1

--- a/solution.py
+++ b/solution.py
@@ -8,6 +8,7 @@
 from jax.sharding import PartitionSpec as P
 
 LANES = 128
+PAIR = 256
 MESH = pl.DeviceIdType.MESH
 F32 = jnp.float32
 BF16 = jnp.bfloat16
@@ -47,7 +48,6 @@
     f2,
     u2,
     g2,
-    out,
     x,
     leafs,
     trees,
@@ -65,7 +65,6 @@
     op_far,
     load_sem,
     x_sem,
-    out_sem,
     ring_send,
     ring_recv,
     fold_send,
@@ -75,7 +74,9 @@
     mixer_send,
     mixer_recv,
 ):
-    chunks, rows, _ = x.shape
+    rows, columns = x.shape
+    chunks = columns // LANES
+    pairs = columns // PAIR
     width = trees.shape[1]
     share = width // ring_size
     half = ring_size // 2
@@ -104,14 +105,7 @@
         )
         for i, (source, place) in enumerate(places):
             loads.append(pltpu.make_async_copy(source, place, load_sem.at[p, i]))
-    x_loads = [
-        pltpu.make_async_copy(
-            matrix.at[:, pl.ds(c * LANES, LANES)], x.at[c], x_sem.at[c]
-        )
-        for c in range(chunks)
-    ]
-    for copy in loads[:4] + x_loads + loads[4:]:
-        copy.start()
+    x_load = pltpu.make_async_copy(matrix, x, x_sem)
 
     barrier = pltpu.get_barrier_semaphore()
 
@@ -131,20 +125,27 @@
     def _():
         greet(parent, k)
 
-    pl.semaphore_wait(barrier, 2 + steps + jnp.where(not_root, 1, 0))
+    for copy in loads[:4] + [x_load] + loads[4:]:
+        copy.start()
+    with jax.named_scope("barrier"):
+        pl.semaphore_wait(barrier, 2 + steps + jnp.where(not_root, 1, 0))
+
+    starts = ((0, 2 * LANES), (2 * LANES, rows - LANES), (0, width), (width, width))
 
     def hops(piece, way):
-        return half if piece == way else half - 1
+        return half if piece % 2 == way else half - 1
 
     def ring_copy(p, piece, way, hop, sent):
         back = hop - 1 if sent else hop
         shard = lax.rem(k + (ring_size - back if way == 0 else back), ring_size)
         row = pl.ds(pl.multiple_of(shard * share, share), share)
-        if piece == 0:
-            first = pl.multiple_of(((shard * share) // LANES) * LANES, LANES)
-            ref = leafs.at[p, row, pl.ds(first, rows + LANES)]
+        start, size = starts[piece]
+        if piece < 2:
+            first = ((shard * share) // LANES) * LANES
+            lanes = pl.ds(pl.multiple_of(first + start, LANES), size)
+            ref = leafs.at[p, row, lanes]
         else:
-            ref = trees.at[p, row, :]
+            ref = trees.at[p, row, pl.ds(start, size)]
         return pltpu.make_async_remote_copy(
             src_ref=ref,
             dst_ref=ref,
@@ -155,17 +156,18 @@
         )
 
     def relay(p, hop):
-        for piece in range(2):
+        for piece in range(4):
             for way in range(2):
                 if hop <= hops(piece, way):
                     if hop > 1:
                         ring_copy(p, piece, way, hop - 1, False).wait_recv()
                     ring_copy(p, piece, way, hop, True).start()
 
-    def gathered(p, piece):
-        for way in range(2):
-            if hops(piece, way) > 0:
-                ring_copy(p, piece, way, hops(piece, way), False).wait_recv()
+    def gathered(p, pieces):
+        for piece in pieces:
+            for way in range(2):
+                if hops(piece, way) > 0:
+                    ring_copy(p, piece, way, hops(piece, way), False).wait_recv()
 
     def top_copy(p, level, c, stride):
         return pltpu.make_async_remote_copy(
@@ -201,6 +203,9 @@
         folds[p, c] = times(op_ut, tops[p, steps, c])
         fold_copy(p, c, steps).start()
 
+    def chunks_of(pair):
+        return range(pair * (PAIR // LANES), (pair + 1) * (PAIR // LANES))
+
     def each_chunk(body):
         def step(c, carry):
             body(c)
@@ -225,41 +230,48 @@
 
     def panel(p, offset):
         block = pl.ds(pl.multiple_of(offset, width), width)
-        gathered(p, 0)
-        prepare_leaf(p, offset)
+        with jax.named_scope("wait_vectors"):
+            gathered(p, (0, 1))
+        with jax.named_scope("prepare_leaf"):
+            prepare_leaf(p, offset)
         if p == 0:
-            for copy in x_loads:
-                copy.wait()
-
-        def leaf(c):
-            before = x[c]
-            mixed = times(op_f, times(op_vt, before))
-            x[c] = before - times(op_v, mixed)
-            tops[p, 0, c] = x[c, block, :]
-
-            @pl.when(steps > 0)
-            def _():
-                top_copy(p, 0, c, 1).start()
-
-        each_chunk(leaf)
-        gathered(p, 1)
+            x_load.wait()
+
+        with jax.named_scope("leaf"):
+            for pair in range(pairs):
+                lanes = pl.ds(pair * PAIR, PAIR)
+                before = x[:, lanes]
+                mixed = times(op_f, times(op_vt, before))
+                x[:, lanes] = before - times(op_v, mixed)
+                for c in chunks_of(pair):
+                    tops[p, 0, c] = x[block, pl.ds(c * LANES, LANES)]
+
+                    @pl.when(steps > 0)
+                    def _():
+                        top_copy(p, 0, c, 1).start()
+        with jax.named_scope("wait_merges"):
+            gathered(p, (2, 3))
 
         @pl.when(not_root)
         def _():
             mixer_copy(p, steps).start()
 
-        prepare_tree(p)
+        with jax.named_scope("prepare_tree"):
+            prepare_tree(p)
 
         @pl.when(steps == 0)
         def _():
-            each_chunk(functools.partial(fold, p))
+            with jax.named_scope("first_fold"):
+                each_chunk(functools.partial(fold, p))
 
         def level_step(level, stride):
-            mixer_copy(p, level).wait_recv()
+            with jax.named_scope("wait_mixer"):
+                mixer_copy(p, level).wait_recv()
             op_far[...] = left_operand(lower_triangle(far_mixers[p, level]))
 
             def upper(c):
-                fold_copy(p, c, level).wait_recv()
+                with jax.named_scope("wait_fold"):
+                    fold_copy(p, c, level).wait_recv()
                 before = tops[p, level, c]
                 weight = times(op_far, before + far_folds[p, level, c])
                 tops[p, level + 1, c] = before - weight
@@ -278,56 +290,54 @@
 
                     @pl.when(level == hop - 2)
                     def _():
-                        relay(1, hop)
+                        with jax.named_scope("relay"):
+                            relay(1, hop)
 
             return stride * 2
 
         lax.fori_loop(0, steps, level_step, jnp.int32(1))
-
-        def lower(c):
-            top_copy(p, 0, c, 0).wait_recv()
-            weight = times(op_g, far_tops[p, c] + folds[p, c])
-            x[c, pl.ds(0, width), :] = tops[p, steps, c] - times(op_u, weight)
-
-        def root(c):
-            x[c, block, :] = tops[p, levels, c]
 
         @pl.when(not_root)
         def _():
-            each_chunk(lower)
+            for pair in range(pairs):
+                both = chunks_of(pair)
+                with jax.named_scope("wait_top"):
+                    for c in both:
+                        top_copy(p, 0, c, 0).wait_recv()
+                gained = [far_tops[p, c] + folds[p, c] for c in both]
+                weight = times(op_g, jnp.concatenate(gained, axis=1))
+                lost = times(op_u, weight)
+                before = [tops[p, steps, c] for c in both]
+                x[pl.ds(0, width), pl.ds(pair * PAIR, PAIR)] = (
+                    jnp.concatenate(before, axis=1) - lost
+                )
 
         @pl.when(d == 0)
         def _():
-            each_chunk(root)
+            for c in range(chunks):
+                x[block, pl.ds(c * LANES, LANES)] = tops[p, levels, c]
 
         if p == 0:
             for hop in range(2, half + 1):
 
                 @pl.when(steps <= hop - 2)
                 def _():
-                    relay(1, hop)
+                    with jax.named_scope("relay"):
+                        relay(1, hop)
 
     for copy in loads[:4]:
         copy.wait()
     for hop in range(1, half + 1):
-        relay(0, hop)
+        with jax.named_scope("ring"):
+            relay(0, hop)
     for copy in loads[4:]:
         copy.wait()
     relay(1, 1)
     panel(0, jnp.int32(0))
     panel(1, jnp.where(d == 0, width, 0))
 
-    stores = [
-        pltpu.make_async_copy(
-            x.at[c], out.at[:, pl.ds(c * LANES, LANES)], out_sem.at[c]
-        )
-        for c in range(chunks)
-    ]
-    for copy in stores:
-        copy.start()
-
     for p in range(2):
-        for piece in range(2):
+        for piece in range(4):
             for way in range(2):
                 for hop in range(1, hops(piece, way) + 1):
                     ring_copy(p, piece, way, hop, True).wait_send()
@@ -342,9 +352,6 @@
         def _():
             mixer_copy(p, steps).wait_send()
             each_chunk(lambda c: fold_copy(p, c, steps).wait_send())
-
-    for copy in stores:
-        copy.wait()
 
 
 def local(levels, ring_size, matrix, *reflectors):
@@ -354,16 +361,16 @@
     chunks = cols // LANES
     half = ring_size // 2
     vmem, dma = pltpu.VMEM, pltpu.SemaphoreType.DMA
-    anywhere = pl.BlockSpec(memory_space=pl.ANY)
+    anywhere = pl.BlockSpec(memory_space=pltpu.HBM)
     tile = (chunks, width, LANES)
     flops = 2 * 3 * 2 * cols * width * (3 * rows + 9 * width)
+    arrays = (matrix, *turned)
     return pl.pallas_call(
         functools.partial(kernel, levels, ring_size),
         out_shape=jax.ShapeDtypeStruct(matrix.shape, matrix.dtype),
         in_specs=[anywhere] * 9,
-        out_specs=anywhere,
+        out_specs=pl.BlockSpec(memory_space=pltpu.VMEM),
         scratch_shapes=[
-            vmem((chunks, rows, LANES), F32),
             vmem((2, width, rows + width), F32),
             vmem((2, width, 2 * width), F32),
             vmem((2, levels, width, width), F32),
@@ -379,10 +386,9 @@
             vmem((width, 3 * width), BF16),
             vmem((width, 3 * width), BF16),
             dma((2, 4)),
-            dma((chunks,)),
-            dma((chunks,)),
-            dma((2, 2, 2, half)),
-            dma((2, 2, 2, half)),
+            dma(()),
+            dma((2, 4, 2, half)),
+            dma((2, 4, 2, half)),
             dma((2, chunks)),
             dma((2, levels, chunks)),
             dma((2, levels, chunks)),
@@ -391,13 +397,13 @@
             dma((2, levels)),
         ],
         compiler_params=pltpu.CompilerParams(
-            collective_id=0, has_side_effects=True, vmem_limit_bytes=48 * 2**20
+            collective_id=0, has_side_effects=True, vmem_limit_bytes=50_331_648
         ),
         cost_estimate=pl.CostEstimate(
             flops=flops, bytes_accessed=8 * rows * cols, transcendentals=0
         ),
         name="tree_update",
-    )(matrix, *turned)
+    )(*(pltpu.with_memory_space_constraint(a, pltpu.HBM) for a in arrays))
 
 
 def solution(mesh):

time: 111 us -> 98.4 us (0.89)
  local copies, waits for them, and re-layouts: 8.42 us -> 0.97 us
  Pallas kernels: 102 us -> 97.3 us
    unnamed x19 -> x1, local copies, waits for them, and re-layouts: 8.42 us -> 0.97 us
    pallas_call x1, Pallas kernels: 102 us -> 97.3 us  [local(): pl.pallas_call(functools.partial(kernel, levels, ring_size), out_shape=ja...]
where the time goes in v2:
time: 98.4 us; the launch traced here: 98.3 us
  Pallas kernels  97.3 us (99%)
    pallas_call x1, Pallas kernels, local(): pl.pallas_call(functools.partial(kernel, levels, ring_size), out_shape=ja...  97.3 us

profile of v2, /device:TPU:32, one launch (start us, length us, event | category | flops | bytes accessed | tf_op | source)
XLA Modules:
  0.0 98.3 jit_solution(12574112295630452162)
XLA Ops:
  0.0 97.3 %tree_update.1 = f32[512,512]{1,0:T(8,128)S(1)} custom-call(f32[512,512]{1,0:T(8,128)} %matrix.1, f32[32,512]{1,0:T(8,128)} %bitcast.8, f32[32,256]{1,0:T(8,128)} %bitcast.10, f32[32,256]{1,0:T(8,128)} %bitcast.11, f32[32,256]{1,0:T(8,128)} %bitcast.12, f32[32,512]{1,0:T(8,128)} %bitcast.9, f32[32,256]{1,0:T(8,128)} %bitcast.13, f32[32,256]{1,0:T(8,128)} %bitcast.14, ...), custom_call_target="tpu_custom_call" | custom-call | flops 6039797760 | bytes 2097152 | tf_op jit(solution)/shard_map/tree_update/pallas_call | solution.py:368
  97.3 1.0 copy.11

commit v3 on v2

--- a/solution.py
+++ b/solution.py
@@ -265,26 +265,8 @@
                 each_chunk(functools.partial(fold, p))
 
         def level_step(level, stride):
-            with jax.named_scope("wait_mixer"):
-                mixer_copy(p, level).wait_recv()
-            op_far[...] = left_operand(lower_triangle(far_mixers[p, level]))
-
-            def upper(c):
-                with jax.named_scope("wait_fold"):
-                    fold_copy(p, c, level).wait_recv()
-                before = tops[p, level, c]
-                weight = times(op_far, before + far_folds[p, level, c])
-                tops[p, level + 1, c] = before - weight
-
-                @pl.when(level + 1 < steps)
-                def _():
-                    top_copy(p, level + 1, c, stride * 2).start()
-
-                @pl.when((level + 1 == steps) & not_root)
-                def _():
-                    fold(p, c)
-
-            each_chunk(upper)
+            prepare_far(p, level, 0)
+            each_chunk(functools.partial(upper, p, level, stride, 0))
             if p == 0:
                 for hop in range(2, half + 1):
 
@@ -295,35 +277,66 @@
 
             return stride * 2
 
-        lax.fori_loop(0, steps, level_step, jnp.int32(1))
-
-        @pl.when(not_root)
-        def _():
-            for pair in range(pairs):
-                both = chunks_of(pair)
-                with jax.named_scope("wait_top"):
-                    for c in both:
-                        top_copy(p, 0, c, 0).wait_recv()
-                gained = [far_tops[p, c] + folds[p, c] for c in both]
-                weight = times(op_g, jnp.concatenate(gained, axis=1))
-                lost = times(op_u, weight)
-                before = [tops[p, steps, c] for c in both]
-                x[pl.ds(0, width), pl.ds(pair * PAIR, PAIR)] = (
-                    jnp.concatenate(before, axis=1) - lost
-                )
-
-        @pl.when(d == 0)
-        def _():
-            for c in range(chunks):
-                x[block, pl.ds(c * LANES, LANES)] = tops[p, levels, c]
-
-        if p == 0:
-            for hop in range(2, half + 1):
-
-                @pl.when(steps <= hop - 2)
+        near = max(levels - 3, 0)
+        lax.fori_loop(0, jnp.minimum(steps, near), level_step, jnp.int32(1))
+
+        @pl.when(steps > near)
+        def _():
+            prepare_far(p, near, 0)
+
+            @pl.when(steps > near + 1)
+            def _():
+                prepare_far(p, near + 1, 1)
+
+            def two_levels(c):
+                upper(p, near, 2**near, 0, c)
+
+                @pl.when(steps > near + 1)
                 def _():
-                    with jax.named_scope("relay"):
-                        relay(1, hop)
+                    upper(p, near + 1, 2 ** (near + 1), 1, c)
+
+            each_chunk(two_levels)
+
+    def prepare_far(p, level, slot):
+        with jax.named_scope("wait_mixer"):
+            mixer_copy(p, level).wait_recv()
+        op_far[slot] = left_operand(lower_triangle(far_mixers[p, level]))
+
+    def upper(p, level, stride, slot, c):
+        with jax.named_scope("wait_fold"):
+            fold_copy(p, c, level).wait_recv()
+        before = tops[p, level, c]
+        weight = times(op_far.at[slot], before + far_folds[p, level, c])
+        tops[p, level + 1, c] = before - weight
+
+        @pl.when(level + 1 < steps)
+        def _():
+            top_copy(p, level + 1, c, stride * 2).start()
+
+        @pl.when((level + 1 == steps) & not_root)
+        def _():
+            fold(p, c)
+
+    def lower(p):
+        for pair in range(pairs):
+            both = chunks_of(pair)
+            with jax.named_scope("wait_top"):
+                for c in both:
+                    top_copy(p, 0, c, 0).wait_recv()
+            gained = [far_tops[p, c] + folds[p, c] for c in both]
+            weight = times(op_g, jnp.concatenate(gained, axis=1))
+            lost = times(op_u, weight)
+            before = [tops[p, steps, c] for c in both]
+            x[pl.ds(0, width), pl.ds(pair * PAIR, PAIR)] = (
+                jnp.concatenate(before, axis=1) - lost
+            )
+
+    def root(p, first):
+        last = levels - 1
+        prepare_far(p, last, 0)
+        for c in range(chunks):
+            upper(p, last, 2**last, 0, c)
+            x[pl.ds(first, width), pl.ds(c * LANES, LANES)] = tops[p, levels, c]
 
     for copy in loads[:4]:
         copy.wait()
@@ -334,7 +347,28 @@
         copy.wait()
     relay(1, 1)
     panel(0, jnp.int32(0))
-    panel(1, jnp.where(d == 0, width, 0))
+
+    @pl.when(not_root)
+    def _():
+        lower(0)
+
+    for hop in range(2, half + 1):
+
+        @pl.when(jnp.minimum(steps, max(levels - 3, 0)) <= hop - 2)
+        def _():
+            with jax.named_scope("relay"):
+                relay(1, hop)
+
+    panel(1, jnp.where(not_root, 0, width))
+
+    @pl.when(not_root)
+    def _():
+        lower(1)
+
+    @pl.when(d == 0)
+    def _():
+        root(0, 0)
+        root(1, width)
 
     for p in range(2):
         for piece in range(4):
@@ -384,7 +418,7 @@
             vmem((width, 3 * width), BF16),
             vmem((width, 3 * width), BF16),
             vmem((width, 3 * width), BF16),
-            vmem((width, 3 * width), BF16),
+            vmem((2, width, 3 * width), BF16),
             dma((2, 4)),
             dma(()),
             dma((2, 4, 2, half)),

time: 98.4 us -> 97.3 us (0.989)
  the two profiles are of different devices: /device:TPU:32 before, /device:TPU:64 now
where the time goes in v3:
time: 97.3 us; the launch traced here: 97.2 us
  Pallas kernels  96.3 us (99%)
    pallas_call x1, Pallas kernels, local(): pl.pallas_call(functools.partial(kernel, levels, ring_size), out_shape=ja...  96.3 us

profile of v3, /device:TPU:64, one launch (start us, length us, event | category | flops | bytes accessed | tf_op | source)
XLA Modules:
  0.0 97.2 jit_solution(16356535902692708493)
XLA Ops:
  0.0 96.3 %tree_update.1 = f32[512,512]{1,0:T(8,128)S(1)} custom-call(f32[512,512]{1,0:T(8,128)} %matrix.1, f32[32,512]{1,0:T(8,128)} %bitcast.8, f32[32,256]{1,0:T(8,128)} %bitcast.10, f32[32,256]{1,0:T(8,128)} %bitcast.11, f32[32,256]{1,0:T(8,128)} %bitcast.12, f32[32,512]{1,0:T(8,128)} %bitcast.9, f32[32,256]{1,0:T(8,128)} %bitcast.13, f32[32,256]{1,0:T(8,128)} %bitcast.14, ...), custom_call_target="tpu_custom_call" | custom-call | flops 6039797760 | bytes 2097152 | tf_op jit(solution)/shard_map/tree_update/pallas_call | solution.py:402
  96.3 1.0 %copy.11 = f32[512,512]{1,0:T(8,128)} copy(f32[512,512]{1,0:T(8,128)S(1)} %tree_update.1) | data formatting | bytes 2097152

commit v4 on v3

--- a/solution.py
+++ b/solution.py
@@ -9,6 +9,7 @@
 
 LANES = 128
 PAIR = 256
+CHAINED = (2, 4, 5)
 MESH = pl.DeviceIdType.MESH
 F32 = jnp.float32
 BF16 = jnp.bfloat16
@@ -56,6 +57,7 @@
     far_folds,
     folds,
     far_tops,
+    passed,
     op_v,
     op_vt,
     op_f,
@@ -71,6 +73,7 @@
     fold_recv,
     top_send,
     top_recv,
+    pass_send,
     mixer_send,
     mixer_recv,
 ):
@@ -93,6 +96,14 @@
         reach = reach + one * 2**i
     not_root = d != 0
     parent = d - reach
+    hands_on = jnp.int32(0)
+    handed = jnp.int32(0)
+    for i in CHAINED:
+        if i < levels:
+            hands_on = hands_on + jnp.where(lax.rem(d, 2 ** (i + 1)) == 2 ** (i - 1), 1, 0)
+            handed = handed + jnp.where(lax.rem(d, 2 ** (i + 1)) == 2**i, 1, 0)
+    before_me = d - reach // 2
+    after_me = d + reach
 
     own = pl.ds(pl.multiple_of(k * share, share), share)
     loads = []
@@ -125,10 +136,20 @@
     def _():
         greet(parent, k)
 
+    @pl.when(hands_on > 0)
+    def _():
+        greet(after_me, k)
+
+    @pl.when(handed > 0)
+    def _():
+        greet(before_me, k)
+
     for copy in loads[:4] + [x_load] + loads[4:]:
         copy.start()
     with jax.named_scope("barrier"):
-        pl.semaphore_wait(barrier, 2 + steps + jnp.where(not_root, 1, 0))
+        pl.semaphore_wait(
+            barrier, 2 + steps + jnp.where(not_root, 1, 0) + hands_on + handed
+        )
 
     starts = ((0, 2 * LANES), (2 * LANES, rows - LANES), (0, width), (width, width))
 
@@ -179,6 +200,22 @@
             device_id_type=MESH,
         )
 
+    def pass_copy(p, c):
+        return pltpu.make_async_remote_copy(
+            src_ref=passed.at[p, c],
+            dst_ref=far_tops.at[p, c],
+            send_sem=pass_send.at[p, c],
+            recv_sem=top_recv.at[p, c],
+            device_id=(after_me, k),
+            device_id_type=MESH,
+        )
+
+    def sends_top(level):
+        sends = level < steps
+        for i in CHAINED:
+            sends = sends & (level != i)
+        return sends
+
     def fold_copy(p, c, level):
         return pltpu.make_async_remote_copy(
             src_ref=folds.at[p, c],
@@ -268,7 +305,7 @@
             prepare_far(p, level, 0)
             each_chunk(functools.partial(upper, p, level, stride, 0))
             if p == 0:
-                for hop in range(2, half + 1):
+                for hop in range(3, half + 1):
 
                     @pl.when(level == hop - 2)
                     def _():
@@ -276,6 +313,10 @@
                             relay(1, hop)
 
             return stride * 2
+
+        if p == 0 and half > 1:
+            with jax.named_scope("relay"):
+                relay(1, 2)
 
         near = max(levels - 3, 0)
         lax.fori_loop(0, jnp.minimum(steps, near), level_step, jnp.int32(1))
@@ -309,7 +350,7 @@
         weight = times(op_far.at[slot], before + far_folds[p, level, c])
         tops[p, level + 1, c] = before - weight
 
-        @pl.when(level + 1 < steps)
+        @pl.when(sends_top(level + 1))
         def _():
             top_copy(p, level + 1, c, stride * 2).start()
 
@@ -318,17 +359,19 @@
             fold(p, c)
 
     def lower(p):
-        for pair in range(pairs):
-            both = chunks_of(pair)
+        for c in range(chunks):
             with jax.named_scope("wait_top"):
-                for c in both:
-                    top_copy(p, 0, c, 0).wait_recv()
-            gained = [far_tops[p, c] + folds[p, c] for c in both]
-            weight = times(op_g, jnp.concatenate(gained, axis=1))
-            lost = times(op_u, weight)
-            before = [tops[p, steps, c] for c in both]
-            x[pl.ds(0, width), pl.ds(pair * PAIR, PAIR)] = (
-                jnp.concatenate(before, axis=1) - lost
+                top_copy(p, 0, c, 0).wait_recv()
+            upper_rows = far_tops[p, c]
+            weight = times(op_g, upper_rows + folds[p, c])
+
+            @pl.when(hands_on > 0)
+            def _():
+                passed[p, c] = upper_rows - weight
+                pass_copy(p, c).start()
+
+            x[pl.ds(0, width), pl.ds(c * LANES, LANES)] = (
+                tops[p, steps, c] - times(op_u, weight)
             )
 
     def root(p, first):
@@ -352,7 +395,7 @@
     def _():
         lower(0)
 
-    for hop in range(2, half + 1):
+    for hop in range(3, half + 1):
 
         @pl.when(jnp.minimum(steps, max(levels - 3, 0)) <= hop - 2)
         def _():
@@ -377,10 +420,17 @@
                     ring_copy(p, piece, way, hop, True).wait_send()
 
         def sent_tops(level, carry):
-            each_chunk(lambda c: top_copy(p, level, c, 0).wait_send())
+            @pl.when(sends_top(level))
+            def _():
+                each_chunk(lambda c: top_copy(p, level, c, 0).wait_send())
+
             return carry
 
         lax.fori_loop(0, steps, sent_tops, 0)
+
+        @pl.when(hands_on > 0)
+        def _():
+            each_chunk(lambda c: pass_copy(p, c).wait_send())
 
         @pl.when(not_root)
         def _():
@@ -412,6 +462,7 @@
             vmem((2, levels, *tile), F32),
             vmem((2, *tile), F32),
             vmem((2, *tile), F32),
+            vmem((2, *tile), F32),
             vmem((rows, 3 * width), BF16),
             vmem((width, 3 * rows), BF16),
             vmem((width, 3 * width), BF16),
@@ -427,6 +478,7 @@
             dma((2, levels, chunks)),
             dma((2, levels, chunks)),
             dma((2, chunks)),
+            dma((2, chunks)),
             dma((2,)),
             dma((2, levels)),
         ],

time: 97.3 us -> 91.1 us (0.936)
  Pallas kernels: 96.3 us -> 90 us
    pallas_call x1, Pallas kernels: 96.3 us -> 90 us  [local(): pl.pallas_call(functools.partial(kernel, levels, ring_size), out_shape=ja...]
where the time goes in v4:
time: 91.1 us; the launch traced here: 91 us
  Pallas kernels  90 us (99%)
  local copies, waits for them, and re-layouts  0.97 us (1%)
    pallas_call x1, Pallas kernels, local(): pl.pallas_call(functools.partial(kernel, levels, ring_size), out_shape=ja...  90 us

profile of v4, /device:TPU:64, one launch (start us, length us, event | category | flops | bytes accessed | tf_op | source)
XLA Modules:
  0.0 91.0 jit_solution(8221869390935882667)
XLA Ops:
  0.0 90.0 %tree_update.1 = f32[512,512]{1,0:T(8,128)S(1)} custom-call(f32[512,512]{1,0:T(8,128)} %matrix.1, f32[32,512]{1,0:T(8,128)} %bitcast.8, f32[32,256]{1,0:T(8,128)} %bitcast.10, f32[32,256]{1,0:T(8,128)} %bitcast.11, f32[32,256]{1,0:T(8,128)} %bitcast.12, f32[32,512]{1,0:T(8,128)} %bitcast.9, f32[32,256]{1,0:T(8,128)} %bitcast.13, f32[32,256]{1,0:T(8,128)} %bitcast.14, ...), custom_call_target="tpu_custom_call" | custom-call | flops 6039797760 | bytes 2097152 | tf_op jit(solution)/shard_map/tree_update/pallas_call | solution.py:452
  90.0 1.0 %copy.11 = f32[512,512]{1,0:T(8,128)} copy(f32[512,512]{1,0:T(8,128)S(1)} %tree_update.1) | data formatting | bytes 2097152

commit v5 on v4

--- a/solution.py
+++ b/solution.py
@@ -236,9 +236,14 @@
             device_id_type=MESH,
         )
 
+    late = steps == levels - 1
+
     def fold(p, c):
         folds[p, c] = times(op_ut, tops[p, steps, c])
-        fold_copy(p, c, steps).start()
+
+        @pl.when((p > 0) | jnp.logical_not(late))
+        def _():
+            fold_copy(p, c, steps).start()
 
     def chunks_of(pair):
         return range(pair * (PAIR // LANES), (pair + 1) * (PAIR // LANES))
@@ -274,8 +279,8 @@
         if p == 0:
             x_load.wait()
 
-        with jax.named_scope("leaf"):
-            for pair in range(pairs):
+        for pair in range(pairs):
+            with jax.named_scope("leaf"):
                 lanes = pl.ds(pair * PAIR, PAIR)
                 before = x[:, lanes]
                 mixed = times(op_f, times(op_vt, before))
@@ -286,12 +291,20 @@
                     @pl.when(steps > 0)
                     def _():
                         top_copy(p, 0, c, 1).start()
-        with jax.named_scope("wait_merges"):
-            gathered(p, (2, 3))
-
-        @pl.when(not_root)
-        def _():
-            mixer_copy(p, steps).start()
+
+            if pair == 0:
+                with jax.named_scope("wait_merges"):
+                    gathered(p, (2, 3))
+
+                @pl.when(not_root)
+                def _():
+                    mixer_copy(p, steps).start()
+
+        if p == 1:
+
+            @pl.when(late)
+            def _():
+                each_chunk(lambda c: fold_copy(0, c, steps).start())
 
         with jax.named_scope("prepare_tree"):
             prepare_tree(p)
@@ -305,7 +318,7 @@
             prepare_far(p, level, 0)
             each_chunk(functools.partial(upper, p, level, stride, 0))
             if p == 0:
-                for hop in range(3, half + 1):
+                for hop in range(2, half + 1):
 
                     @pl.when(level == hop - 2)
                     def _():
@@ -313,10 +326,6 @@
                             relay(1, hop)
 
             return stride * 2
-
-        if p == 0 and half > 1:
-            with jax.named_scope("relay"):
-                relay(1, 2)
 
         near = max(levels - 3, 0)
         lax.fori_loop(0, jnp.minimum(steps, near), level_step, jnp.int32(1))
@@ -391,13 +400,24 @@
     relay(1, 1)
     panel(0, jnp.int32(0))
 
+    early = (steps == 2) & (levels > 4)
+    if half > 3:
+
+        @pl.when(early)
+        def _():
+            with jax.named_scope("relay"):
+                relay(1, 4)
+
     @pl.when(not_root)
     def _():
         lower(0)
 
-    for hop in range(3, half + 1):
-
-        @pl.when(jnp.minimum(steps, max(levels - 3, 0)) <= hop - 2)
+    for hop in range(2, half + 1):
+        due = jnp.minimum(steps, max(levels - 3, 0)) <= hop - 2
+        if hop == 4:
+            due = due & jnp.logical_not(early)
+
+        @pl.when(due)
         def _():
             with jax.named_scope("relay"):
                 relay(1, hop)

time: 91.1 us -> 90.8 us (level)
  the two profiles are of different devices: /device:TPU:64 before, /device:TPU:48 now
where the time goes in v5:
time: 90.8 us; the launch traced here: 90.7 us
  Pallas kernels  89.8 us (99%)
  local copies, waits for them, and re-layouts  0.97 us (1%)
    pallas_call x1, Pallas kernels, local(): pl.pallas_call(functools.partial(kernel, levels, ring_size), out_shape=ja...  89.8 us

profile of v5, /device:TPU:48, one launch (start us, length us, event | category | flops | bytes accessed | tf_op | source)
XLA Modules:
  0.0 90.7 jit_solution(5773677751625763285)
XLA Ops:
  0.0 89.8 %tree_update.1 = f32[512,512]{1,0:T(8,128)S(1)} custom-call(f32[512,512]{1,0:T(8,128)} %matrix.1, f32[32,512]{1,0:T(8,128)} %bitcast.8, f32[32,256]{1,0:T(8,128)} %bitcast.10, f32[32,256]{1,0:T(8,128)} %bitcast.11, f32[32,256]{1,0:T(8,128)} %bitcast.12, f32[32,512]{1,0:T(8,128)} %bitcast.9, f32[32,256]{1,0:T(8,128)} %bitcast.13, f32[32,256]{1,0:T(8,128)} %bitcast.14, ...), custom_call_target="tpu_custom_call" | custom-call | flops 6039797760 | bytes 2097152 | tf_op jit(solution)/shard_map/tree_update/pallas_call | solution.py:472
  89.8 1.0 %copy.11 = f32[512,512]{1,0:T(8,128)} copy(f32[512,512]{1,0:T(8,128)S(1)} %tree_update.1) | data formatting | bytes 2097152

commit v6 on v5

--- a/solution.py
+++ b/solution.py
@@ -300,12 +300,6 @@
                 def _():
                     mixer_copy(p, steps).start()
 
-        if p == 1:
-
-            @pl.when(late)
-            def _():
-                each_chunk(lambda c: fold_copy(0, c, steps).start())
-
         with jax.named_scope("prepare_tree"):
             prepare_tree(p)
 
@@ -400,22 +394,26 @@
     relay(1, 1)
     panel(0, jnp.int32(0))
 
-    early = (steps == 2) & (levels > 4)
-    if half > 3:
-
-        @pl.when(early)
+    @pl.when(late)
+    def _():
+        each_chunk(lambda c: fold_copy(0, c, steps).start())
+
+    near = max(levels - 3, 0)
+    for hop in range(2, min(half, near + 2) + 1):
+
+        @pl.when(steps == hop - 2)
         def _():
             with jax.named_scope("relay"):
-                relay(1, 4)
+                relay(1, hop)
 
     @pl.when(not_root)
     def _():
         lower(0)
 
     for hop in range(2, half + 1):
-        due = jnp.minimum(steps, max(levels - 3, 0)) <= hop - 2
-        if hop == 4:
-            due = due & jnp.logical_not(early)
+        due = jnp.minimum(steps, near) <= hop - 2
+        if hop <= near + 2:
+            due = due & (steps != hop - 2)
 
         @pl.when(due)
         def _():

time: 90.8 us -> 86.6 us (0.954)
  the two profiles are of different devices: /device:TPU:48 before, /device:TPU:64 now
where the time goes in v6:
time: 86.6 us; the launch traced here: 86.5 us
  Pallas kernels  85.5 us (99%)
  local copies, waits for them, and re-layouts  0.97 us (1%)
    pallas_call x1, Pallas kernels, local(): pl.pallas_call(functools.partial(kernel, levels, ring_size), out_shape=ja...  85.5 us

profile of v6, /device:TPU:64, one launch (start us, length us, event | category | flops | bytes accessed | tf_op | source)
XLA Modules:
  0.0 86.5 jit_solution(12821944739092805154)
XLA Ops:
  0.0 85.5 %tree_update.1 = f32[512,512]{1,0:T(8,128)S(1)} custom-call(f32[512,512]{1,0:T(8,128)} %matrix.1, f32[32,512]{1,0:T(8,128)} %bitcast.8, f32[32,256]{1,0:T(8,128)} %bitcast.10, f32[32,256]{1,0:T(8,128)} %bitcast.11, f32[32,256]{1,0:T(8,128)} %bitcast.12, f32[32,512]{1,0:T(8,128)} %bitcast.9, f32[32,256]{1,0:T(8,128)} %bitcast.13, f32[32,256]{1,0:T(8,128)} %bitcast.14, ...), custom_call_target="tpu_custom_call" | custom-call | flops 6039797760 | bytes 2097152 | tf_op jit(solution)/shard_map/tree_update/pallas_call | solution.py:470
  85.5 1.0 %copy.11 = f32[512,512]{1,0:T(8,128)} copy(f32[512,512]{1,0:T(8,128)S(1)} %tree_update.1) | data formatting | bytes 2097152

commit v7 on v6

--- a/solution.py
+++ b/solution.py
@@ -384,6 +384,25 @@
             upper(p, last, 2**last, 0, c)
             x[pl.ds(first, width), pl.ds(c * LANES, LANES)] = tops[p, levels, c]
 
+    def sent(p):
+        def sent_tops(level, carry):
+            @pl.when(sends_top(level))
+            def _():
+                each_chunk(lambda c: top_copy(p, level, c, 0).wait_send())
+
+            return carry
+
+        lax.fori_loop(0, steps, sent_tops, 0)
+
+        @pl.when(hands_on > 0)
+        def _():
+            each_chunk(lambda c: pass_copy(p, c).wait_send())
+
+        @pl.when(not_root)
+        def _():
+            mixer_copy(p, steps).wait_send()
+            each_chunk(lambda c: fold_copy(p, c, steps).wait_send())
+
     for copy in loads[:4]:
         copy.wait()
     for hop in range(1, half + 1):
@@ -422,38 +441,23 @@
 
     panel(1, jnp.where(not_root, 0, width))
 
-    @pl.when(not_root)
-    def _():
-        lower(1)
-
-    @pl.when(d == 0)
-    def _():
-        root(0, 0)
-        root(1, width)
-
     for p in range(2):
         for piece in range(4):
             for way in range(2):
                 for hop in range(1, hops(piece, way) + 1):
                     ring_copy(p, piece, way, hop, True).wait_send()
-
-        def sent_tops(level, carry):
-            @pl.when(sends_top(level))
-            def _():
-                each_chunk(lambda c: top_copy(p, level, c, 0).wait_send())
-
-            return carry
-
-        lax.fori_loop(0, steps, sent_tops, 0)
-
-        @pl.when(hands_on > 0)
-        def _():
-            each_chunk(lambda c: pass_copy(p, c).wait_send())
-
-        @pl.when(not_root)
-        def _():
-            mixer_copy(p, steps).wait_send()
-            each_chunk(lambda c: fold_copy(p, c, steps).wait_send())
+    sent(0)
+
+    @pl.when(not_root)
+    def _():
+        lower(1)
+
+    @pl.when(d == 0)
+    def _():
+        root(0, 0)
+        root(1, width)
+
+    sent(1)
 
 
 def local(levels, ring_size, matrix, *reflectors):

time: 86.6 us -> 86.3 us (level)
  no operation moved by 1% of the time
where the time goes in v7:
time: 86.3 us; the launch traced here: 86.2 us
  Pallas kernels  85.2 us (99%)
  local copies, waits for them, and re-layouts  0.97 us (1%)
    pallas_call x1, Pallas kernels, local(): pl.pallas_call(functools.partial(kernel, levels, ring_size), out_shape=ja...  85.2 us

profile of v7, /device:TPU:64, one launch (start us, length us, event | category | flops | bytes accessed | tf_op | source)
XLA Modules:
  0.0 86.2 jit_solution(4493816172299420868)
XLA Ops:
  0.0 85.2 %tree_update.1 = f32[512,512]{1,0:T(8,128)S(1)} custom-call(f32[512,512]{1,0:T(8,128)} %matrix.1, f32[32,512]{1,0:T(8,128)} %bitcast.8, f32[32,256]{1,0:T(8,128)} %bitcast.10, f32[32,256]{1,0:T(8,128)} %bitcast.11, f32[32,256]{1,0:T(8,128)} %bitcast.12, f32[32,512]{1,0:T(8,128)} %bitcast.9, f32[32,256]{1,0:T(8,128)} %bitcast.13, f32[32,256]{1,0:T(8,128)} %bitcast.14, ...), custom_call_target="tpu_custom_call" | custom-call | flops 6039797760 | bytes 2097152 | tf_op jit(solution)/shard_map/tree_update/pallas_call | solution.py:474
  85.2 1.0 %copy.11 = f32[512,512]{1,0:T(8,128)} copy(f32[512,512]{1,0:T(8,128)S(1)} %tree_update.1) | data formatting | bytes 2097152
